TPU v7x, 256 devices: a whole 4x4x8 slice. The times are simulated.
256 devices in a mesh: row: 32 (over x, y, core), col: 8 (over z).
Axes of the slice: x: 4, y: 4, z: 8, core: 2. Of those that a mesh axis runs over, the one named last changes fastest.
Arguments:
- matrix: float32 [5120, 5120], P('row', 'col'), may hold values from -64 to 64
Outputs:
- iterate: float32 [5120, 5120], P('row', 'col')
- trace_value: float32 [2], replicated
- frobenius: float32 [2], replicated
All inputs are finite; a program needn't handle non-finite values.
Results may differ from a plain program's by a relative error of at most 0.003.
Values may be sent and summed in bfloat16 or wider, within the bound.
No kernel may reach another device: no remote copies, remote signals or barrier semaphores. Data moves between devices by JAX's collectives and lax.ppermute only.
A program may use at most 64 MiB of HBM per device.

v0:
```python
import jax
import jax.numpy as jnp
from jax import lax
from jax.sharding import Mesh
from jax.sharding import PartitionSpec as P

ITERS = 2
ROW = ("row_0", "row_1", "row_2")
ROW_COL = ("row_0", "row_1", "row_2", "col")
target = 0.0625


def from_everyone(shard, axis):
    peers = lax.axis_size(axis)
    return lax.all_to_all(
        jnp.broadcast_to(shard[None], (peers, *shard.shape)), axis, 0, 0, tiled=True
    )


def in_order(pieces, dim):
    shape = list(pieces.shape[1:])
    shape[dim] *= pieces.shape[0]
    return jnp.moveaxis(pieces, 0, dim).reshape(shape)


def collect(shard, axis, dim):
    pieces = from_everyone(shard, axis)
    return in_order(pieces, dim)


def over_axes(shard, axes):
    for axis in axes:
        shard = lax.psum(shard, axis)
    return shard


def add_rows(portion, right_panel):
    return jnp.dot(portion, right_panel, preferred_element_type=jnp.float32)


def on_device(matrix):
    rounded = matrix.astype(jnp.bfloat16)
    current = rounded.astype(jnp.float32)
    row_ids = lax.axis_index(ROW) * matrix.shape[0] + lax.broadcasted_iota(
        jnp.int32, matrix.shape, 0
    )
    col_ids = lax.axis_index("col") * matrix.shape[1] + lax.broadcasted_iota(
        jnp.int32, matrix.shape, 1
    )
    on_diagonal = row_ids == col_ids
    traces = []
    norms = []
    for step in range(ITERS):
        row_panel = collect(rounded, "col", 1)
        if step == 0:
            order_full = row_panel.shape[1]
            squares = over_axes(jnp.sum(current * current), ROW_COL)
            scale = target * order_full / (squares + 1e-06)
            root = jnp.sqrt(scale)
        else:
            scale = jnp.float32(1.0)
            root = jnp.float32(1.0)
        kept_panel = lax.all_gather(rounded, ROW, axis=0, tiled=True)
        product = jnp.dot(row_panel, kept_panel, preferred_element_type=jnp.float32)
        squared = (product * scale).astype(jnp.bfloat16)
        cubic_part = add_rows(
            lax.all_gather(squared, "col", axis=1, tiled=True), right_panel=kept_panel
        )
        current = root * (1.5 * current - 0.5 * cubic_part)
        rounded = current.astype(jnp.bfloat16)
        diagonal_part = jnp.sum(jnp.where(on_diagonal, current, 0.0))
        square_part = jnp.sum(current * current)
        trace_now, total_now = (over_axes(diagonal_part, ROW_COL), over_axes(square_part, ROW_COL))
        traces.append(trace_now)
        norms.append(jnp.sqrt(total_now))
    return (current, jnp.stack(traces), jnp.stack(norms))


def solution(mesh):
    split = Mesh(
        mesh.devices.reshape(4, 4, 2, mesh.shape["col"]), ("row_0", "row_1", "row_2", "col")
    )
    return jax.shard_map(
        on_device,
        mesh=split,
        in_specs=(P(ROW, "col"),),
        out_specs=(P(ROW, "col"), P(), P()),
        check_vma=False,
    )
```

profile of v0, /device:TPU:32, one launch (start us, length us, event | category | flops | bytes accessed | tf_op | source)
XLA Modules:
  0.0 274.8 jit_solution(13605825605742799116)
XLA Ops:
  7.2 0.0 all-gather.5.cloned.1.call-start
  7.2 2.3 fusion.4
  9.5 0.0 all-gather.5.cloned.1.call-update
  9.5 2.2 broadcast_in_dim.9
  11.8 8.6 %all-to-all-start = ((bf16[8,160,640]{2,1,0:T(8,128)(2,1)}), bf16[8,160,640]{2,1,0:T(8,128)(2,1)S(1)}, u32[]{:S(2)}, u32[]{:S(2)}) async-start(bf16[8,160,640]{2,1,0:T(8,128)(2,1)} %broadcast_in_dim.9), calls=%async_computation | async-start | bytes 3276800 | tf_op jit(solution)/shard_map/all_to_all | solution.py:15
  20.3 0.0 all-gather.7.cloned.1.call-start
  20.4 11.1 %psum.140 = f32[]{:T(128)} all-reduce(f32[]{:T(128)} %get-tuple-element.23), channel_id=1, replica_groups=mesh['row_0'=4,'row_1'=4,'row_2'=2,'col'=8] {'row_0'}, use_global_device_ids=true, to_apply=%region_1.0 | all-reduce | flops 1 | bytes 8 | tf_op jit(solution)/shard_map/psum | solution.py:33
  31.5 11.4 %psum.141 = f32[]{:T(128)} all-reduce(f32[]{:T(128)} %psum.140), channel_id=1, replica_groups=mesh['row_0'=4,'row_1'=4,'row_2'=2,'col'=8] {'row_1'}, use_global_device_ids=true, to_apply=%region_2.0 | all-reduce | flops 1 | bytes 8 | tf_op jit(solution)/shard_map/psum | solution.py:33
  42.8 3.1 %psum.142 = f32[]{:T(128)} all-reduce(f32[]{:T(128)} %psum.141), channel_id=1, replica_groups=mesh['row_0'=4,'row_1'=4,'row_2'=2,'col'=8] {'row_2'}, use_global_device_ids=true, to_apply=%region_3.0 | all-reduce | flops 1 | bytes 8 | tf_op jit(solution)/shard_map/psum | solution.py:33
  45.9 20.6 %psum.143 = f32[]{:T(128)} all-reduce(f32[]{:T(128)} %psum.142), channel_id=1, replica_groups=mesh['row_0'=4,'row_1'=4,'row_2'=2,'col'=8] {'col'}, use_global_device_ids=true, to_apply=%region_4.0 | all-reduce | flops 1 | bytes 8 | tf_op jit(solution)/shard_map/psum | solution.py:33
  67.2 0.0 all-to-all-done
  67.2 0.2 copy.6
  67.5 0.7 all-gather.5.cloned.1.call-done
  68.2 0.0 copy-start
  68.2 5.0 %fusion.3 = bf16[160,640]{1,0:T(8,128)(2,1)} fusion(bf16[160,5120]{1,0:T(8,128)(2,1)S(1)} %bitcast.18, bf16[5120,640]{1,0:T(8,128)(2,1)} %all-gather.5.cloned.1.call-done, f32[]{:T(128)S(6)} %div.3), kind=kOutput, calls=%fused_computation.6 | convolution fusion | flops 1048780800 | bytes 8396804 | tf_op jit(solution)/shard_map/dot_general | solution.py:64
  73.2 0.0 all-gather.7.cloned.1.call-update
  73.2 0.0 all-gather.9.cloned.1.call-start
  73.3 41.0 %all-gather.7.cloned.1.call-done = bf16[160,5120]{1,0:T(8,128)(2,1)} async-done(((bf16[160,640]{1,0:T(8,128)(2,1)}), bf16[160,5120]{1,0:T(8,128)(2,1)}) %all-gather.7.cloned.1.call-update) | async-done | bytes 1638416 | tf_op jit(solution)/shard_map/all_gather | solution.py:67
  114.3 0.0 copy-done
  114.3 6.1 %multiply_reduce_fusion.1 = (f32[]{:T(128)}, f32[]{:T(128)}, bf16[160,640]{1,0:T(8,128)(2,1)}, f32[160,640]{1,0:T(8,128)S(1)}) fusion(s32[640]{0:T(1024)S(1)} %iota_add_fusion, s32[160]{0:T(256)S(1)} %iota_add_fusion.1, bf16[160,5120]{1,0:T(8,128)(2,1)} %all-gather.7.cloned.1.call-done, bf16[5120,640]{1,0:T(8,128)(2,1)} %all-gather.5.cloned.1.call-done, ...), kind=kOutput, calls=%fused_computation.16 | convolution fusion | flops 1049702400 | bytes 9014412 | tf_op jit(solution)/shard_map/dot_general | solution.py:38
  120.5 0.0 all-gather.9.cloned.1.call-update
  120.5 0.0 all-gather.11.cloned.1.call-start
  120.5 1.1 broadcast_in_dim.18
  121.6 40.6 %all_to_all.10 = bf16[8,160,640]{2,1,0:T(8,128)(2,1)S(1)} all-to-all(bf16[8,160,640]{2,1,0:T(8,128)(2,1)S(1)} %broadcast_in_dim.18), channel_id=1, replica_groups=mesh['row_0'=4,'row_1'=4,'row_2'=2,'col'=8] {'col'}, dimensions={0} | all-to-all | bytes 3276800 | tf_op jit(solution)/shard_map/all_to_all | solution.py:15
  162.2 0.2 copy.7
  162.4 11.6 %all-gather.9.cloned.1.call-done = bf16[5120,640]{1,0:T(8,128)(2,1)} async-done(((bf16[160,640]{1,0:T(8,128)(2,1)}), bf16[5120,640]{1,0:T(8,128)(2,1)}) %all-gather.9.cloned.1.call-update) | async-done | bytes 6553616 | tf_op jit(solution)/shard_map/all_gather | solution.py:63
  174.0 5.0 %convolution_convert_fusion = bf16[160,640]{1,0:T(8,128)(2,1)} fusion(bf16[160,5120]{1,0:T(8,128)(2,1)S(1)} %bitcast.19, bf16[5120,640]{1,0:T(8,128)(2,1)} %all-gather.9.cloned.1.call-done), kind=kOutput, calls=%fused_computation.7 | convolution fusion | flops 1048678400 | bytes 8396800 | tf_op jit(solution)/shard_map/dot_general | solution.py:64
  179.0 0.0 all-gather.11.cloned.1.call-update
  179.0 38.3 %all-gather.11.cloned.1.call-done = bf16[160,5120]{1,0:T(8,128)(2,1)} async-done(((bf16[160,640]{1,0:T(8,128)(2,1)}), bf16[160,5120]{1,0:T(8,128)(2,1)}) %all-gather.11.cloned.1.call-update) | async-done | bytes 1638416 | tf_op jit(solution)/shard_map/all_gather | solution.py:67
  217.3 6.2 %multiply_reduce_fusion = (f32[]{:T(128)}, f32[]{:T(128)}, f32[160,640]{1,0:T(8,128)}) fusion(s32[640]{0:T(1024)S(1)} %iota_add_fusion, s32[160]{0:T(256)S(1)} %iota_add_fusion.1, bf16[160,5120]{1,0:T(8,128)(2,1)} %all-gather.11.cloned.1.call-done, bf16[5120,640]{1,0:T(8,128)(2,1)} %all-gather.9.cloned.1.call-done, f32[160,640]{1,0:T(8,128)S(1)} %get-tuple-element.26), kind=kOutput, calls=%fused_computation.15 | convolution fusion | flops 1049395200 | bytes 9014408 | tf_op jit(solution)/shard_map/dot_general | solution.py:38
  223.5 11.1 %all-reduce.2 = (f32[]{:T(128)}, f32[]{:T(128)}, f32[]{:T(128)}, f32[]{:T(128)}) all-reduce(f32[]{:T(128)} %get-tuple-element.6, f32[]{:T(128)} %get-tuple-element.4, f32[]{:T(128)} %get-tuple-element.5, f32[]{:T(128)} %get-tuple-element.3), channel_id=1, replica_groups=mesh['row_0'=4,'row_1'=4,'row_2'=2,'col'=8] {'row_0'}, use_global_device_ids=true, to_apply=%region_11.12 | all-reduce | flops 4 | bytes 32 | tf_op jit(solution)/shard_map/psum | solution.py:33
  234.6 11.1 %all-reduce.1 = (f32[]{:T(128)}, f32[]{:T(128)}, f32[]{:T(128)}, f32[]{:T(128)}) all-reduce(f32[]{:T(128)} %get-tuple-element.15, f32[]{:T(128)} %get-tuple-element.16, f32[]{:T(128)} %get-tuple-element.17, f32[]{:T(128)} %get-tuple-element.18), channel_id=1, replica_groups=mesh['row_0'=4,'row_1'=4,'row_2'=2,'col'=8] {'row_1'}, use_global_device_ids=true, to_apply=%region_12.13 | all-reduce | flops 4 | bytes 32 | tf_op jit(solution)/shard_map/psum | solution.py:33
  245.7 3.2 %all-reduce.3 = (f32[]{:T(128)}, f32[]{:T(128)}, f32[]{:T(128)}, f32[]{:T(128)}) all-reduce(f32[]{:T(128)} %get-tuple-element.11, f32[]{:T(128)} %get-tuple-element.12, f32[]{:T(128)} %get-tuple-element.13, f32[]{:T(128)} %get-tuple-element.14), channel_id=1, replica_groups=mesh['row_0'=4,'row_1'=4,'row_2'=2,'col'=8] {'row_2'}, use_global_device_ids=true, to_apply=%region_13.14 | all-reduce | flops 4 | bytes 32 | tf_op jit(solution)/shard_map/psum | solution.py:33
  248.9 16.1 %all-reduce = (f32[1]{0:T(128)}, f32[1]{0:T(128)}, f32[]{:T(128)}, f32[]{:T(128)}) all-reduce(f32[1]{0:T(128)} %bitcast.3, f32[1]{0:T(128)} %bitcast.2, f32[]{:T(128)} %get-tuple-element.21, f32[]{:T(128)} %get-tuple-element.22), channel_id=1, replica_groups=mesh['row_0'=4,'row_1'=4,'row_2'=2,'col'=8] {'col'}, use_global_device_ids=true, to_apply=%region_14.15 | all-reduce | flops 4 | bytes 32 | tf_op jit(solution)/shard_map/psum | solution.py:33
  266.4 1.9 pad_maximum_fusion
  (2 shorter events, 0.0 us)
Async XLA Ops:
  7.2 61.0 %all-gather.5.cloned.1.call-start = ((), (), s32[]{:S(2)}) async-start(), calls=%async_computation.2 | async-start | bytes 6758400 | tf_op jit(solution)/shard_map/all_gather | solution.py:63
  11.8 55.4 %all-to-all-start = ((bf16[8,160,640]{2,1,0:T(8,128)(2,1)}), bf16[8,160,640]{2,1,0:T(8,128)(2,1)S(1)}, u32[]{:S(2)}, u32[]{:S(2)}) async-start(bf16[8,160,640]{2,1,0:T(8,128)(2,1)} %broadcast_in_dim.9), calls=%async_computation | async-start | bytes 3276800 | tf_op jit(solution)/shard_map/all_to_all | solution.py:15
  20.3 94.0 %all-gather.7.cloned.1.call-start = ((), (), s32[]{:S(2)}) async-start(), calls=%async_computation.3 | async-start | bytes 1843200 | tf_op jit(solution)/shard_map/all_gather | solution.py:67
  68.2 46.2 %copy-start = (bf16[160,640]{1,0:T(8,128)(2,1)S(1)}, bf16[160,640]{1,0:T(8,128)(2,1)}, u32[]{:S(2)}) copy-start(bf16[160,640]{1,0:T(8,128)(2,1)} %get-tuple-element.24) | copy-start | bytes 614404
  73.2 100.8 %all-gather.9.cloned.1.call-start = ((), (), s32[]{:S(2)}) async-start(), calls=%async_computation.4 | async-start | bytes 6758400 | tf_op jit(solution)/shard_map/all_gather | solution.py:63
  120.5 96.8 %all-gather.11.cloned.1.call-start = ((), (), s32[]{:S(2)}) async-start(), calls=%async_computation.5 | async-start | bytes 1843200 | tf_op jit(solution)/shard_map/all_gather | solution.py:67
Sparse Core Ops, SparseCore 0:
  11.1 57.0 all-gather.4
  73.3 40.9 all-gather.6
  120.6 53.3 all-gather.8
  179.2 38.0 all-gather.10
where the time goes:
time: 275 us
  blocking collectives  128 us (47%)
  waiting for transfers between devices  91.6 us (33%)
  matrix products  22.3 us (8%)
  between operations  15.9 us (6%)
  starting transfers between devices  8.69 us (3%)
  other arithmetic  4.18 us (2%)
  local copies, waits for them, and re-layouts  3.75 us (1%)
    psum x8, blocking collectives, over_axes(): shard = lax.psum(shard, axis)  87.7 us
    all_gather x2, waiting for transfers between devices, on_device(): lax.all_gather(squared, 'col', axis=1, tiled=True)  79.2 us
    all_to_all x1, blocking collectives, from_everyone(): lax.all_to_all(jnp.broadcast_to(shard[None], (peers, *shard.shape)), axis...  40.6 us
    dot_general x2, matrix products, add_rows(): return jnp.dot(portion, right_panel, preferred_element_type=jnp.float32)  12.3 us
    all_gather x2, waiting for transfers between devices, on_device(): kept_panel = lax.all_gather(rounded, ROW, axis=0, tiled=True)  12.3 us
    dot_general x2, matrix products, on_device(): product = jnp.dot(row_panel, kept_panel, preferred_element_type=jnp.float32)  10 us
    all_to_all x1, starting transfers between devices, from_everyone(): lax.all_to_all(jnp.broadcast_to(shard[None], (peers, *shard.shape)), axis...  8.57 us
  transfers between devices with their start and end apart: 5, of which 4 were waited for; matrix products, arithmetic and copies ran while one was open for 1% of the time, Pallas kernels for 0%

commit v1 on v0

--- a/solution.py
+++ b/solution.py
@@ -30,7 +30,7 @@
 
 def over_axes(shard, axes):
     for axis in axes:
-        shard = lax.psum(shard, axis)
+        shard = jnp.sum(lax.all_gather(shard, axis), axis=0)
     return shard
 
 

time: 275 us -> 302 us (1.098)
  local copies, waits for them, and re-layouts: 3.75 us -> 33.5 us
  other arithmetic: 4.18 us -> 16.2 us
  blocking collectives: 128 us -> 119 us
  waiting for transfers between devices: 91.6 us -> 85.6 us
    psum x8 -> x0, blocking collectives: 87.7 us -> none  [over_axes(): shard = lax.psum(shard, axis)]
    unnamed x0 -> x8, blocking collectives: none -> 77.9 us
    unnamed x2 -> x54, local copies, waits for them, and re-layouts: 0.01 us -> 29.8 us
    reduce_sum x0 -> x20, other arithmetic: none -> 12.1 us  [over_axes(): shard = jnp.sum(lax.all_gather(shard, axis), axis=0)]
    all_gather x2, waiting for transfers between devices: 79.2 us -> 73.9 us  [on_device(): lax.all_gather(squared, 'col', axis=1, tiled=True)]
  transfers between devices with their start and end apart: 5 -> 5, of which waited for: 4 -> 3; matrix products, arithmetic and copies ran while one was open for 1% -> 6% of each run, Pallas kernels for 0% -> 0%
where the time goes in v1:
time: 302 us; the launch traced here: 301 us
  blocking collectives  119 us (39%)
  waiting for transfers between devices  85.6 us (28%)
  local copies, waits for them, and re-layouts  33.5 us (11%)
  matrix products  22.4 us (7%)
  other arithmetic  16.2 us (5%)
  between operations  16 us (5%)
  starting transfers between devices  8.84 us (3%)
    unnamed x8, blocking collectives  77.9 us
    all_gather x2, waiting for transfers between devices, on_device(): lax.all_gather(squared, 'col', axis=1, tiled=True)  73.9 us
    all_to_all x1, blocking collectives, from_everyone(): lax.all_to_all(jnp.broadcast_to(shard[None], (peers, *shard.shape)), axis...  40.6 us
    unnamed x54, local copies, waits for them, and re-layouts  29.8 us
    dot_general x2, matrix products, add_rows(): return jnp.dot(portion, right_panel, preferred_element_type=jnp.float32)  12.3 us
    reduce_sum x20, other arithmetic, over_axes(): shard = jnp.sum(lax.all_gather(shard, axis), axis=0)  12.1 us
    all_gather x2, waiting for transfers between devices, on_device(): kept_panel = lax.all_gather(rounded, ROW, axis=0, tiled=True)  11.6 us
    dot_general x2, matrix products, on_device(): product = jnp.dot(row_panel, kept_panel, preferred_element_type=jnp.float32)  10.1 us
  transfers between devices with their start and end apart: 5, of which 3 were waited for; matrix products, arithmetic and copies ran while one was open for 6% of the time, Pallas kernels for 0%

profile of v1, /device:TPU:32, one launch (start us, length us, event | category | flops | bytes accessed | tf_op | source)
XLA Modules:
  0.0 301.1 jit_solution(14554605420120814608)
XLA Ops:
  7.2 2.3 fusion.4
  9.5 2.2 broadcast_in_dim.9
  11.8 8.7 %all-to-all-start = ((bf16[8,160,640]{2,1,0:T(8,128)(2,1)}), bf16[8,160,640]{2,1,0:T(8,128)(2,1)S(1)}, u32[]{:S(2)}, u32[]{:S(2)}) async-start(bf16[8,160,640]{2,1,0:T(8,128)(2,1)} %broadcast_in_dim.9), calls=%async_computation | async-start | bytes 3276800 | tf_op jit(solution)/shard_map/all_to_all | solution.py:15
  21.1 1.4 dynamic-update-slice
  22.5 10.5 %all-reduce = f32[4]{0:T(128)S(1)} all-reduce(f32[4]{0:T(128)S(1)} %dynamic-update-slice), channel_id=1, replica_groups=mesh['row_0'=4,'row_1'=4,'row_2'=2,'col'=8] {'row_0'}, use_global_device_ids=true, to_apply=%add | all-reduce | flops 4 | bytes 32
  33.0 0.6 dynamic-slice.1
  33.6 0.6 reduce_sum.226
  34.2 1.4 dynamic-update-slice.1
  35.5 10.7 %all-reduce.1 = f32[4]{0:T(128)S(1)} all-reduce(f32[4]{0:T(128)S(1)} %dynamic-update-slice.1), channel_id=1, replica_groups=mesh['row_0'=4,'row_1'=4,'row_2'=2,'col'=8] {'row_1'}, use_global_device_ids=true, to_apply=%add.1 | all-reduce | flops 4 | bytes 32
  46.3 0.6 dynamic-slice.2
  46.9 0.6 reduce_sum.227
  47.5 1.3 dynamic-update-slice.2
  48.8 2.4 all-reduce.2
  51.2 0.6 dynamic-slice.3
  51.8 0.6 reduce_sum.228
  52.4 1.4 dynamic-update-slice.3
  53.8 15.6 %all-reduce.3 = f32[8]{0:T(128)S(1)} all-reduce(f32[8]{0:T(128)S(1)} %dynamic-update-slice.3), channel_id=1, replica_groups=mesh['row_0'=4,'row_1'=4,'row_2'=2,'col'=8] {'col'}, use_global_device_ids=true, to_apply=%add.3 | all-reduce | flops 8 | bytes 64
  69.4 0.6 reduce_sum.229
  71.0 5.0 %fusion.3 = bf16[160,640]{1,0:T(8,128)(2,1)} fusion(bf16[160,5120]{1,0:T(8,128)(2,1)S(1)} %bitcast.42, bf16[5120,640]{1,0:T(8,128)(2,1)} %all-gather.5.cloned.1.call-done, f32[]{:T(128)S(6)} %div.3), kind=kOutput, calls=%fused_computation.6 | convolution fusion | flops 1048780800 | bytes 8396804 | tf_op jit(solution)/shard_map/dot_general | solution.py:64
  76.2 38.4 %all-gather.7.cloned.1.call-done = bf16[160,5120]{1,0:T(8,128)(2,1)} async-done(((bf16[160,640]{1,0:T(8,128)(2,1)}), bf16[160,5120]{1,0:T(8,128)(2,1)}) %all-gather.7.cloned.1.call-update) | async-done | bytes 1638416 | tf_op jit(solution)/shard_map/all_gather | solution.py:67
  114.6 6.1 %multiply_reduce_fusion.1 = (f32[]{:T(128)}, f32[]{:T(128)}, bf16[160,640]{1,0:T(8,128)(2,1)}, f32[160,640]{1,0:T(8,128)S(1)}) fusion(s32[640]{0:T(1024)S(1)} %iota_add_fusion, s32[160]{0:T(256)S(1)} %iota_add_fusion.1, bf16[160,5120]{1,0:T(8,128)(2,1)} %all-gather.7.cloned.1.call-done, bf16[5120,640]{1,0:T(8,128)(2,1)} %all-gather.5.cloned.1.call-done, ...), kind=kOutput, calls=%fused_computation.16 | convolution fusion | flops 1049702400 | bytes 9014412 | tf_op jit(solution)/shard_map/dot_general | solution.py:38
  120.8 1.1 broadcast_in_dim.18
  121.9 40.6 %all_to_all.10 = bf16[8,160,640]{2,1,0:T(8,128)(2,1)S(1)} all-to-all(bf16[8,160,640]{2,1,0:T(8,128)(2,1)S(1)} %broadcast_in_dim.18), channel_id=1, replica_groups=mesh['row_0'=4,'row_1'=4,'row_2'=2,'col'=8] {'col'}, dimensions={0} | all-to-all | bytes 3276800 | tf_op jit(solution)/shard_map/all_to_all | solution.py:15
  162.7 11.6 %all-gather.9.cloned.1.call-done = bf16[5120,640]{1,0:T(8,128)(2,1)} async-done(((bf16[160,640]{1,0:T(8,128)(2,1)}), bf16[5120,640]{1,0:T(8,128)(2,1)}) %all-gather.9.cloned.1.call-update) | async-done | bytes 6553616 | tf_op jit(solution)/shard_map/all_gather | solution.py:63
  174.3 5.0 %convolution_convert_fusion = bf16[160,640]{1,0:T(8,128)(2,1)} fusion(bf16[160,5120]{1,0:T(8,128)(2,1)S(1)} %bitcast.43, bf16[5120,640]{1,0:T(8,128)(2,1)} %all-gather.9.cloned.1.call-done), kind=kOutput, calls=%fused_computation.7 | convolution fusion | flops 1048678400 | bytes 8396800 | tf_op jit(solution)/shard_map/dot_general | solution.py:64
  179.4 1.4 dynamic-update-slice.4
  180.7 1.4 dynamic-update-slice.12
  182.2 35.5 %all-gather.11.cloned.1.call-done = bf16[160,5120]{1,0:T(8,128)(2,1)} async-done(((bf16[160,640]{1,0:T(8,128)(2,1)}), bf16[160,5120]{1,0:T(8,128)(2,1)}) %all-gather.11.cloned.1.call-update) | async-done | bytes 1638416 | tf_op jit(solution)/shard_map/all_gather | solution.py:67
  217.6 6.2 %multiply_reduce_fusion = (f32[]{:T(128)}, f32[]{:T(128)}, f32[160,640]{1,0:T(8,128)}) fusion(s32[640]{0:T(1024)S(1)} %iota_add_fusion, s32[160]{0:T(256)S(1)} %iota_add_fusion.1, bf16[160,5120]{1,0:T(8,128)(2,1)} %all-gather.11.cloned.1.call-done, bf16[5120,640]{1,0:T(8,128)(2,1)} %all-gather.9.cloned.1.call-done, f32[160,640]{1,0:T(8,128)S(1)} %get-tuple-element.26), kind=kOutput, calls=%fused_computation.15 | convolution fusion | flops 1049395200 | bytes 9014408 | tf_op jit(solution)/shard_map/dot_general | solution.py:38
  223.8 1.4 dynamic-update-slice.8
  225.2 1.4 dynamic-update-slice.16
  226.6 10.4 %all-reduce.22 = (f32[4]{0:T(128)S(1)}, f32[4]{0:T(128)S(1)}, f32[4]{0:T(128)S(1)}, f32[4]{0:T(128)S(1)}) all-reduce(f32[4]{0:T(128)S(1)} %dynamic-update-slice.8, f32[4]{0:T(128)S(1)} %dynamic-update-slice.4, f32[4]{0:T(128)S(1)} %dynamic-update-slice.16, ...), channel_id=1, replica_groups=mesh['row_0'=4,'row_1'=4,'row_2'=2,'col'=8] {'row_0'}, use_global_device_ids=true, to_apply=%add.8 | all-reduce | flops 16 | bytes 128
  237.0 0.6 reduce_sum.236
  237.6 1.4 dynamic-update-slice.9
  239.0 0.6 reduce_sum.231
  239.6 1.4 dynamic-update-slice.5
  241.0 0.6 reduce_sum.246
  241.6 1.4 dynamic-update-slice.17
  242.9 0.6 reduce_sum.241
  243.5 1.4 dynamic-update-slice.13
  244.9 10.4 %all-reduce.21 = (f32[4]{0:T(128)S(1)}, f32[4]{0:T(128)S(1)}, f32[4]{0:T(128)S(1)}, f32[4]{0:T(128)S(1)}) all-reduce(f32[4]{0:T(128)S(1)} %dynamic-update-slice.9, f32[4]{0:T(128)S(1)} %dynamic-update-slice.5, f32[4]{0:T(128)S(1)} %dynamic-update-slice.17, ...), channel_id=1, replica_groups=mesh['row_0'=4,'row_1'=4,'row_2'=2,'col'=8] {'row_1'}, use_global_device_ids=true, to_apply=%add.9 | all-reduce | flops 16 | bytes 128
  255.4 0.6 reduce_sum.237
  256.0 1.3 dynamic-update-slice.10
  257.3 0.6 reduce_sum.232
  257.9 1.3 dynamic-update-slice.6
  259.2 0.6 reduce_sum.247
  259.8 1.3 dynamic-update-slice.18
  261.2 0.6 reduce_sum.242
  261.8 1.3 dynamic-update-slice.14
  263.1 2.4 all-reduce.23
  265.5 0.6 reduce_sum.238
  266.1 1.4 dynamic-update-slice.11
  267.5 0.6 reduce_sum.233
  268.1 1.4 dynamic-update-slice.7
  269.5 0.6 reduce_sum.248
  270.1 1.4 dynamic-update-slice.19
  271.5 0.6 reduce_sum.243
  272.1 1.4 dynamic-update-slice.15
  273.4 15.4 %all-reduce.20 = (f32[8]{0:T(128)S(1)}, f32[8]{0:T(128)S(1)}, f32[8]{0:T(128)S(1)}, f32[8]{0:T(128)S(1)}) all-reduce(f32[8]{0:T(128)S(1)} %dynamic-update-slice.11, f32[8]{0:T(128)S(1)} %dynamic-update-slice.7, f32[8]{0:T(128)S(1)} %dynamic-update-slice.19, ...), channel_id=1, replica_groups=mesh['row_0'=4,'row_1'=4,'row_2'=2,'col'=8] {'col'}, use_global_device_ids=true, to_apply=%add.11 | all-reduce | flops 32 | bytes 256
  288.9 0.6 reduce_sum.249
  290.2 0.6 reduce_sum.244
  291.5 0.7 reduce_sum.239
  292.1 0.6 reduce_sum.234
  292.7 1.8 pad_maximum_fusion
  (45 shorter events, 1.3 us)
Async XLA Ops:
  7.2 63.8 %all-gather.5.cloned.1.call-start = ((), (), s32[]{:S(2)}) async-start(), calls=%async_computation.2 | async-start | bytes 6758400 | tf_op jit(solution)/shard_map/all_gather | solution.py:63
  11.8 8.7 %copy-start.4 = (u32[256]{0:T(256)S(1)}, u32[256]{0:T(256)}, u32[]{:S(2)}) copy-start(u32[256]{0:T(256)} %constant.38) | copy-start | bytes 3076
  11.8 21.2 %copy-start.3 = (u32[256]{0:T(256)S(1)}, u32[256]{0:T(256)}, u32[]{:S(2)}) copy-start(u32[256]{0:T(256)} %constant.43) | copy-start | bytes 3076
  11.8 34.5 %copy-start.2 = (u32[256]{0:T(256)S(1)}, u32[256]{0:T(256)}, u32[]{:S(2)}) copy-start(u32[256]{0:T(256)} %constant.48) | copy-start | bytes 3076
  11.8 39.4 %copy-start.1 = (u32[256]{0:T(256)S(1)}, u32[256]{0:T(256)}, u32[]{:S(2)}) copy-start(u32[256]{0:T(256)} %constant.53) | copy-start | bytes 3076
  11.8 58.9 %all-to-all-start = ((bf16[8,160,640]{2,1,0:T(8,128)(2,1)}), bf16[8,160,640]{2,1,0:T(8,128)(2,1)S(1)}, u32[]{:S(2)}, u32[]{:S(2)}) async-start(bf16[8,160,640]{2,1,0:T(8,128)(2,1)} %broadcast_in_dim.9), calls=%async_computation | async-start | bytes 3276800 | tf_op jit(solution)/shard_map/all_to_all | solution.py:15
  20.5 94.1 %all-gather.7.cloned.1.call-start = ((), (), s32[]{:S(2)}) async-start(), calls=%async_computation.3 | async-start | bytes 1843200 | tf_op jit(solution)/shard_map/all_gather | solution.py:67
  71.0 43.6 %copy-start = (bf16[160,640]{1,0:T(8,128)(2,1)S(1)}, bf16[160,640]{1,0:T(8,128)(2,1)}, u32[]{:S(2)}) copy-start(bf16[160,640]{1,0:T(8,128)(2,1)} %get-tuple-element.24) | copy-start | bytes 614404
  76.1 98.2 %all-gather.9.cloned.1.call-start = ((), (), s32[]{:S(2)}) async-start(), calls=%async_computation.4 | async-start | bytes 6758400 | tf_op jit(solution)/shard_map/all_gather | solution.py:63
  120.8 96.9 %all-gather.11.cloned.1.call-start = ((), (), s32[]{:S(2)}) async-start(), calls=%async_computation.5 | async-start | bytes 1843200 | tf_op jit(solution)/shard_map/all_gather | solution.py:67
Sparse Core Ops, SparseCore 0:
  11.1 57.0 all-gather.4
  76.2 38.3 all-gather.6
  120.9 53.3 all-gather.8
  179.5 38.0 all-gather.10
